TPU v7x, 32 devices: a whole 2x2x4 slice. The times are simulated.
32 devices in a mesh: rep: 4 (over x, y), dp: 8 (over z, core).
Axes of the slice: x: 2, y: 2, z: 4, core: 2. Of those that a mesh axis runs over, the one named last changes fastest.
Arguments:
- g_w_gate: bfloat16 [32, 2, 1280, 5120], P(('rep', 'dp')), parts along dimension 0
- g_w_up: bfloat16 [32, 2, 1280, 5120], P(('rep', 'dp')), parts along dimension 0
- g_w_down: bfloat16 [32, 2, 5120, 1280], P(('rep', 'dp')), parts along dimension 0
- w_gate: bfloat16 [2, 1280, 5120], replicated
- w_up: bfloat16 [2, 1280, 5120], replicated
- w_down: bfloat16 [2, 5120, 1280], replicated
- m_w_gate: float32 [2, 1280, 5120], P(None, 'dp')
- m_w_up: float32 [2, 1280, 5120], P(None, 'dp')
- m_w_down: float32 [2, 5120, 1280], P(None, 'dp')
- v_w_gate: float32 [2, 1280, 5120], P(None, 'dp')
- v_w_up: float32 [2, 1280, 5120], P(None, 'dp')
- v_w_down: float32 [2, 5120, 1280], P(None, 'dp')
Outputs:
- output 1: bfloat16 [8, 1280, 5120], P('rep'), parts along dimension 0
- output 2: bfloat16 [8, 1280, 5120], P('rep'), parts along dimension 0
- output 3: bfloat16 [8, 5120, 1280], P('rep'), parts along dimension 0
- output 4: float32 [8, 1280, 5120], P('rep', 'dp'), parts along dimension 0
- output 5: float32 [8, 1280, 5120], P('rep', 'dp'), parts along dimension 0
- output 6: float32 [8, 5120, 1280], P('rep', 'dp'), parts along dimension 0
- output 7: float32 [8, 1280, 5120], P('rep', 'dp'), parts along dimension 0
- output 8: float32 [8, 1280, 5120], P('rep', 'dp'), parts along dimension 0
- output 9: float32 [8, 5120, 1280], P('rep', 'dp'), parts along dimension 0
There are 4 independent parts. A program takes and returns all parts, laid end to end along the dimension named above; an argument that names none is the same for every part.
All inputs are finite; a program needn't handle non-finite values.
Results may differ from a plain program's by a relative error of at most 0.022.
Values are sent between devices in bfloat16 or wider.
A program may use at most 2 GiB of HBM per device.

v0:
```python
import jax
import jax.numpy as jnp
from jax import lax
from jax.sharding import PartitionSpec as P


def adamw(w, m, v, g):
    m = 0.9 * m + 0.1 * g
    v = 0.95 * v + 0.05 * g * g
    step = m * lax.rsqrt(v + 1e-8) + 0.1 * w
    return (w - 0.02 * step).astype(jnp.bfloat16), m, v


def clipped(gradients, sum_of_squares, count):
    factor = jnp.minimum(1.0, 0.5 * lax.rsqrt(sum_of_squares / count + 1e-30))
    return [g * factor for g in gradients]


def solution(mesh):
    def step(*arrays):
        terms, weights, m, v = (arrays[i : i + 3] for i in (0, 3, 6, 9))
        gradients = [lax.psum_scatter(t[0], "dp", scatter_dimension=1, tiled=True).astype(jnp.float32) for t in terms]
        squares = lax.psum(sum(jnp.sum(g * g) for g in gradients), "dp")
        gradients = clipped(gradients, squares, lax.psum(1, "dp") * sum(g.size for g in gradients))
        me = lax.axis_index("dp")
        own = [lax.dynamic_slice_in_dim(w, me * one.shape[1], one.shape[1], 1).astype(jnp.float32) for w, one in zip(weights, m, strict=True)]
        new = [adamw(w, m, v, g) for w, m, v, g in zip(own, m, v, gradients, strict=True)]
        whole = [lax.all_gather(one[0], "dp", axis=1, tiled=True) for one in new]
        return (*whole, *(one[1] for one in new), *(one[2] for one in new))

    all_of, cut = P(None, None, None), P(None, "dp", None)
    return jax.shard_map(
        step,
        mesh=mesh,
        in_specs=(P(("rep", "dp"), None, None, None),) * 3 + (all_of,) * 3 + (cut,) * 6,
        out_specs=(P("rep", None, None),) * 3 + (P("rep", "dp", None),) * 6,
        check_vma=False,
    )
```

profile of v0, /device:TPU:0, one launch (start us, length us, event | category | flops | bytes accessed | tf_op | source)
XLA Modules:
  0.0 1566.3 jit_solution(17307797982120936471)
XLA Ops:
  7.2 0.0 reduce-scatter.4.cloned.1.call-start
  7.2 0.7 reduce-scatter.4.cloned.1.call-update
  7.9 0.0 reduce-scatter.6.cloned.1.call-start
  8.0 0.7 reduce-scatter.6.cloned.1.call-update
  8.7 0.0 reduce-scatter.8.cloned.1.call-start
  8.7 0.7 reduce-scatter.8.cloned.1.call-update
  9.4 0.0 all-gather.8.cloned.1.call-start
  9.4 260.4 %reduce-scatter.4.cloned.1.call-done = bf16[2,160,5120]{2,1,0:T(8,128)(2,1)} async-done(((bf16[2,1280,5120]{2,1,0:T(8,128)(2,1)}), bf16[2,160,5120]{2,1,0:T(8,128)(2,1)}) %reduce-scatter.4.cloned.1.call-update) | async-done | bytes 3276816 | tf_op jit(solution)/shard_map/reduce_scatter | solution.py:22
  269.9 4.2 fusion.9
  274.1 253.7 %reduce-scatter.6.cloned.1.call-done = bf16[2,160,5120]{2,1,0:T(8,128)(2,1)} async-done(((bf16[2,1280,5120]{2,1,0:T(8,128)(2,1)}), bf16[2,160,5120]{2,1,0:T(8,128)(2,1)}) %reduce-scatter.6.cloned.1.call-update) | async-done | bytes 3276816 | tf_op jit(solution)/shard_map/reduce_scatter | solution.py:22
  527.8 4.2 fusion.10
  533.3 252.4 %reduce-scatter.8.cloned.1.call-done = bf16[2,640,1280]{2,1,0:T(8,128)(2,1)} async-done(((bf16[2,5120,1280]{2,1,0:T(8,128)(2,1)}), bf16[2,640,1280]{2,1,0:T(8,128)(2,1)}) %reduce-scatter.8.cloned.1.call-update) | async-done | bytes 3276816 | tf_op jit(solution)/shard_map/reduce_scatter | solution.py:22
  785.7 4.2 fusion.11
  790.5 14.3 psum.7
  805.5 13.4 fusion.17
  819.0 0.0 all-gather.8.cloned.1.call-update
  819.0 0.0 all-gather.4.cloned.1.call-start
  819.0 0.0 copy-start.1
  819.1 13.6 fusion.8
  832.7 0.0 all-gather.4.cloned.1.call-update
  832.7 0.0 all-gather.6.cloned.1.call-start
  832.8 0.0 copy-done.1
  832.8 11.4 fusion.14
  844.2 0.0 all-gather.6.cloned.1.call-update
  844.2 202.3 %all-gather.8.cloned.1.call-done = bf16[2,5120,1280]{2,1,0:T(8,128)(2,1)} async-done(((bf16[2,640,1280]{2,1,0:T(8,128)(2,1)}), bf16[2,5120,1280]{2,1,0:T(8,128)(2,1)}) %all-gather.8.cloned.1.call-update) | async-done | bytes 26214416 | tf_op jit(solution)/shard_map/all_gather | solution.py:28
  1046.5 229.8 %all-gather.4.cloned.1.call-done = bf16[2,1280,5120]{2,1,0:T(8,128)(2,1)} async-done(((bf16[2,160,5120]{2,1,0:T(8,128)(2,1)}), bf16[2,1280,5120]{2,1,0:T(8,128)(2,1)}) %all-gather.4.cloned.1.call-update) | async-done | bytes 26214416 | tf_op jit(solution)/shard_map/all_gather | solution.py:28
  1276.3 229.8 %all-gather.6.cloned.1.call-done = bf16[2,1280,5120]{2,1,0:T(8,128)(2,1)} async-done(((bf16[2,160,5120]{2,1,0:T(8,128)(2,1)}), bf16[2,1280,5120]{2,1,0:T(8,128)(2,1)}) %all-gather.6.cloned.1.call-update) | async-done | bytes 26214416 | tf_op jit(solution)/shard_map/all_gather | solution.py:28
  1506.0 0.0 copy-start
  1506.1 22.4 %copy.24 = bf16[2,1280,5120]{2,1,0:T(8,128)(2,1)} copy(bf16[2,1280,5120]{2,1,0:T(8,128)(2,1)} %all-gather.4.cloned.1.call-done) | data formatting | bytes 52428800
  1528.5 3.4 copy-done
  1531.9 9.3 copy.25
  1541.1 18.3 %copy.26 = bf16[2,5120,1280]{2,1,0:T(8,128)(2,1)} copy(bf16[2,5120,1280]{2,1,0:T(8,128)(2,1)} %all-gather.8.cloned.1.call-done) | data formatting | bytes 52428800
Async XLA Ops:
  7.2 262.7 %reduce-scatter.4.cloned.1.call-start = ((), (), s32[]{:S(2)}) async-start(), calls=%async_computation.3 | async-start | bytes 29491200 | tf_op jit(solution)/shard_map/reduce_scatter | solution.py:22
  7.9 519.9 %reduce-scatter.6.cloned.1.call-start = ((), (), s32[]{:S(2)}) async-start(), calls=%async_computation.4 | async-start | bytes 29491200 | tf_op jit(solution)/shard_map/reduce_scatter | solution.py:22
  8.7 777.0 %reduce-scatter.8.cloned.1.call-start = ((), (), s32[]{:S(2)}) async-start(), calls=%async_computation.5 | async-start | bytes 29491200 | tf_op jit(solution)/shard_map/reduce_scatter | solution.py:22
  9.4 1037.1 %all-gather.8.cloned.1.call-start = ((), (), s32[]{:S(2)}) async-start(), calls=%async_computation.8 | async-start | bytes 29491200 | tf_op jit(solution)/shard_map/all_gather | solution.py:28
  819.0 457.3 %all-gather.4.cloned.1.call-start = ((), (), s32[]{:S(2)}) async-start(), calls=%async_computation.6 | async-start | bytes 29491200 | tf_op jit(solution)/shard_map/all_gather | solution.py:28
  819.0 13.7 copy-start.1
  832.7 673.3 %all-gather.6.cloned.1.call-start = ((), (), s32[]{:S(2)}) async-start(), calls=%async_computation.7 | async-start | bytes 29491200 | tf_op jit(solution)/shard_map/all_gather | solution.py:28
  1506.0 25.8 %copy-start = (bf16[2,1280,5120]{2,1,0:T(8,128)(2,1)S(1)}, bf16[2,1280,5120]{2,1,0:T(8,128)(2,1)}, u32[]{:S(2)}) copy-start(bf16[2,1280,5120]{2,1,0:T(8,128)(2,1)} %all-gather.6.cloned.1.call-done) | copy-start | bytes 78643200
Sparse Core Ops, SparseCore 0:
  10.3 259.5 reduce-scatter.3
  272.2 255.4 reduce-scatter.5
  530.1 255.4 reduce-scatter.7
  819.1 227.3 all-gather.7
  1048.5 227.6 all-gather.3
  1278.3 227.6 all-gather.5
where the time goes:
time: 1570 us
  waiting for transfers between devices  1430 us (91%)
  local copies, waits for them, and re-layouts  53.4 us (3%)
  other arithmetic  51.1 us (3%)
  between operations  16.8 us (1%)
    reduce_scatter x3, waiting for transfers between devices, step(): lax.psum_scatter(t[0], 'dp', scatter_dimension=1, tiled=True)  766 us
    all_gather x3, waiting for transfers between devices, step(): whole = [lax.all_gather(one[0], 'dp', axis=1, tiled=True) for one in new]  662 us
    unnamed x7, local copies, waits for them, and re-layouts  53.4 us
    convert_element_type x3, other arithmetic, adamw(): return ((w - 0.02 * step).astype(jnp.bfloat16), m, v)  38.4 us
  transfers between devices with their start and end apart: 6, of which 6 were waited for; matrix products, arithmetic and copies ran while one was open for 2% of the time, Pallas kernels for 0%

commit v1 on v0

v1 whole, which is shorter than its diff:
```python
import functools

import jax
import jax.numpy as jnp
from jax import lax
from jax.experimental import pallas as pl
from jax.experimental.pallas import tpu as pltpu
from jax.sharding import PartitionSpec as P

MESH = pl.DeviceIdType.MESH
F32, BF16 = jnp.float32, jnp.bfloat16


def rows_of(x):
    *lead, r, c = x.shape
    n = len(lead)
    x = x.reshape(*lead, r // 8, 8, c // 128, 128).transpose(*range(n), n, n + 2, n + 1, n + 3)
    return x.reshape(*lead, r * c // 128, 128)


def from_rows(x, r, c):
    *lead, _, _ = x.shape
    n = len(lead)
    x = x.reshape(*lead, r // 8, c // 128, 8, 128).transpose(*range(n), n, n + 2, n + 1, n + 3)
    return x.reshape(*lead, r, c)


class Cfg:
    def __init__(self, rows, ch, skew, ch2, lag):
        self.R, self.CH, self.D, self.CH2, self.L = rows, ch, skew, ch2, lag
        self.SUB = rows // ch
        self.N = 12 * self.SUB
        self.SL = 4
        self.SP = 6
        self.SR = skew + 3
        self.SO = 3
        self.K2 = rows // ch2
        self.M = 6 * self.K2


def add_rows(refs, out, n, step, squares=None):
    def body(i, _):
        at = pl.ds(pl.multiple_of(i * step, step), step)
        total = refs[0][at].astype(F32)
        for r in refs[1:]:
            total = total + r[at].astype(F32)
        total = total.astype(BF16)
        out[at] = total
        if squares is not None:
            g = total.astype(F32)
            squares[...] += jnp.sum((g * g).reshape(step // 8, 8, 128), axis=0)
        return 0

    lax.fori_loop(0, n // step, body, 0)


def kernel(cfg, g0, g1, g2, w0, w1, w2, m0, m1, m2, v0, v1, v2, wt, g_own, g_fwd, factor, own, par, rin, out, sq, sq_in,
           gbuf, wbuf, mbuf, vbuf, nbuf, own_sem, ps, pr, rs, rr, par_credit, rin_credit, sqs, sqr,
           e_sem, c_sem, loc_sem, pown_sem, pfc, pfe, pr2, g1r, re, rc, ld_sem, gl_sem):
    R, CH, D, SUB, N = cfg.R, cfg.CH, cfg.D, cfg.SUB, cfg.N
    SL, SP, SR, SO, CH2, K2, M, L = cfg.SL, cfg.SP, cfg.SR, cfg.SO, cfg.CH2, cfg.K2, cfg.M, cfg.L
    g_in, w_in, m_in, v_in = (g0, g1, g2), (w0, w1, w2), (m0, m1, m2), (v0, v1, v2)
    me = lax.axis_index("dp")
    chip, k = me // 2, lax.rem(me, 2)
    half = chip // 2
    end = (chip == 0) | (chip == 3)
    mid = jnp.logical_not(end)
    my_end, my_mid = 3 * half, 1 + half
    far_mid, far_end = 2 - half, 3 - 3 * half
    partner = {"dp": me + 1 - 2 * k}
    to_c = {"dp": 2 * jnp.where(end, my_mid, far_mid) + k}
    to_e = {"dp": 2 * my_end + k}

    def remote(src, dst, send, recv, device):
        return pltpu.make_async_remote_copy(src_ref=src, dst_ref=dst, send_sem=send, recv_sem=recv, device_id=device, device_id_type=MESH)

    barrier = pltpu.get_barrier_semaphore()
    for i in range(1, 8):
        pl.semaphore_signal(barrier, inc=1, device_id={"dp": lax.rem(me + i, 8)}, device_id_type=MESH)
    pl.semaphore_wait(barrier, 7)

    sq[...] = jnp.zeros_like(sq)

    def block_of(s, b, lane):
        if s == 0:
            return 2 * jnp.where(b == 0, far_mid, far_end) + lane
        return 2 * jnp.where(b == 0, my_mid, my_end) + lane

    def split(i):
        p = i // SUB
        return p // 4, lax.rem(p // 2, 2), lax.rem(p, 2), lax.rem(i, SUB) * CH

    def of_weight(w, refs, do):
        for j in range(3):
            @pl.when(w == j)
            def _():
                do(refs[j])

    def term(ref, s, i, lane):
        w, l, b, off = split(i)
        return ref.at[l, pl.ds(pl.multiple_of(block_of(s, b, lane) * R + off, CH), CH)]

    def load_own(s, i):
        w = i // (4 * SUB)
        of_weight(w, g_in, lambda ref: pltpu.make_async_copy(term(ref, s, i, k), own.at[s, lax.rem(i, SL)], own_sem.at[s, lax.rem(i, SL)]).start())

    def wait_own(s, i):
        pltpu.make_async_copy(g_in[0].at[0, pl.ds(0, CH)], own.at[s, lax.rem(i, SL)], own_sem.at[s, lax.rem(i, SL)]).wait()

    def give(ref, s, i):
        j = lax.rem(i, SP)
        return remote(term(ref, s, i, 1 - k), par.at[s, j], ps.at[s, j], pr.at[s, j], partner)

    def send_given(s, i):
        of_weight(i // (4 * SUB), g_in, lambda ref: give(ref, s, i).start())

    def wait_given(s, i):
        give(g_in[0], s, lax.rem(i, SP)).wait_send()

    def wait_par(s, i):
        give(g_in[0], s, lax.rem(i, SP)).wait_recv()

    def forward(s, i, to_stream, device):
        j, o = lax.rem(i, SR), lax.rem(i, SO)
        return remote(out.at[s, o], rin.at[to_stream, j], rs.at[s, o], rr.at[to_stream, j], device)

    def keep(ref, i):
        w, l, b, off = split(i)
        o = lax.rem(i, SO)
        return pltpu.make_async_copy(out.at[1, o], ref.at[w, l, pl.ds(pl.multiple_of(off, CH), CH)], rs.at[1, o])

    for s in (0, 1):
        for i in range(SL):
            load_own(s, jnp.int32(i))
        for i in range(SP - 2):
            send_given(s, jnp.int32(i))

    def stream(s, i, arrives, leaves):
        wait_own(s, i)
        wait_par(s, i)
        refs = [own.at[s, lax.rem(i, SL)], par.at[s, lax.rem(i, SP)]]
        if arrives is not None:
            remote(out.at[s, 0], rin.at[s, lax.rem(i, SR)], rs.at[s, 0], rr.at[s, lax.rem(i, SR)], partner).wait_recv()
            refs.append(rin.at[s, lax.rem(i, SR)])

        @pl.when(i >= SO)
        def _():
            if leaves is None:
                keep(g_own, i - SO).wait()
            else:
                forward(s, i - SO, leaves[0], leaves[1]).wait_send()

        add_rows(refs, out.at[s, lax.rem(i, SO)], CH, cfg.step, sq if leaves is None else None)

        @pl.when(i + SP < N)
        def _():
            pl.semaphore_signal(par_credit.at[s], inc=1, device_id=partner, device_id_type=MESH)

        if arrives is not None:
            @pl.when(i + SR < N)
            def _():
                pl.semaphore_signal(rin_credit.at[arrives[0]], inc=1, device_id=arrives[1], device_id_type=MESH)

        if leaves is None:
            b = lax.rem(i // SUB, 2)

            @pl.when(b == 0)
            def _():
                keep(g_fwd, i).start()

            @pl.when(b == 1)
            def _():
                keep(g_own, i).start()
        else:
            @pl.when(i >= SR)
            def _():
                pl.semaphore_wait(rin_credit.at[s], 1)

            forward(s, i, leaves[0], leaves[1]).start()

        @pl.when(i + SL < N)
        def _():
            load_own(s, i + SL)

        j = i + SP - 2

        @pl.when(j < N)
        def _():
            @pl.when(j >= SP)
            def _():
                wait_given(s, j - SP)
                pl.semaphore_wait(par_credit.at[s], 1)

            send_given(s, j)

    def hand(t):
        p, off = t // K2, pl.multiple_of(lax.rem(t, K2) * CH2, CH2)
        at = (p // 2, lax.rem(p, 2), pl.ds(off, CH2))
        return remote(g_fwd.at[at], g_own.at[at], e_sem.at[lax.rem(t, 2)], g1r.at[t], to_c)

    def first(t, _):
        i0, i1 = t - jnp.where(end, 0, D), t - jnp.where(end, 3 * D, 2 * D)
        in0, in1 = (i0 >= 0) & (i0 < N), (i1 >= 0) & (i1 < N)

        @pl.when(end & in0)
        def _():
            stream(0, i0, None, (0, to_c))

        @pl.when(mid & in0)
        def _():
            stream(0, i0, (0, to_e), (1, to_c))

        @pl.when(mid & in1)
        def _():
            stream(1, i1, (0, to_c), (1, to_e))

        @pl.when(end & in1)
        def _():
            stream(1, i1, (1, to_c), None)

        @pl.when(end & (t == N + 1))
        def _():
            hand(jnp.int32(0)).start()

        return 0

    lax.fori_loop(0, N + 3 * D, first, 0)

    for i in range(N - SO, N):
        @pl.when(end)
        def _():
            forward(0, jnp.int32(i), 0, to_c).wait_send()
            keep(g_own, jnp.int32(i)).wait()

        @pl.when(mid)
        def _():
            forward(0, jnp.int32(i), 1, to_c).wait_send()
            forward(1, jnp.int32(i), 1, to_e).wait_send()

    part = 2 * half + k

    def tell(i):
        return remote(sq, sq_in.at[part], sqs.at[i], sqr.at[part], {"dp": lax.rem(me + i, 8)})

    @pl.when(end)
    def _():
        for i in (2, 6, 1, 3, 4, 5, 7):
            tell(i).start()

    def loads(t, slot):
        p, off = t // K2, pl.multiple_of(lax.rem(t, K2) * CH2, CH2)
        l = lax.rem(p, 2)

        def start(w):
            pltpu.make_async_copy(w_in[w].at[l, pl.ds(pl.multiple_of(me * R + off, CH2), CH2)], wbuf.at[slot], ld_sem.at[0, slot]).start()
            pltpu.make_async_copy(m_in[w].at[l, pl.ds(off, CH2)], mbuf.at[slot], ld_sem.at[1, slot]).start()
            pltpu.make_async_copy(v_in[w].at[l, pl.ds(off, CH2)], vbuf.at[slot], ld_sem.at[2, slot]).start()

        for w in range(3):
            @pl.when(p // 2 == w)
            def _():
                start(w)

    def wait_loads(slot):
        pltpu.make_async_copy(w_in[0].at[0, pl.ds(0, CH2)], wbuf.at[slot], ld_sem.at[0, slot]).wait()
        pltpu.make_async_copy(m_in[0].at[0, pl.ds(0, CH2)], mbuf.at[slot], ld_sem.at[1, slot]).wait()
        pltpu.make_async_copy(v_in[0].at[0, pl.ds(0, CH2)], vbuf.at[slot], ld_sem.at[2, slot]).wait()

    def load_g(t, slot):
        p, off = t // K2, pl.multiple_of(lax.rem(t, K2) * CH2, CH2)
        return pltpu.make_async_copy(g_own.at[p // 2, lax.rem(p, 2), pl.ds(off, CH2)], gbuf.at[slot], gl_sem.at[slot])

    loads(jnp.int32(0), jnp.int32(0))

    @pl.when(end)
    def _():
        load_g(jnp.int32(0), jnp.int32(0)).start()

    for j in range(4):
        @pl.when(end & (part == j))
        def _():
            sq_in[j] = sq[...]

        @pl.when(jnp.logical_not(end & (part == j)))
        def _():
            remote(sq, sq_in.at[j], sqs.at[0], sqr.at[j], partner).wait_recv()

    total = jnp.sum((sq_in[0] + sq_in[1]) + (sq_in[2] + sq_in[3]))
    factor[...] = jnp.minimum(1.0, 0.5 * lax.rsqrt(jnp.full((8, 128), total, F32) * (1.0 / (48.0 * R * 128)) + 1e-30))

    def at(t, dev):
        p = t // K2
        return wt.at[p // 2, lax.rem(p, 2), pl.ds(pl.multiple_of(dev * R + lax.rem(t, K2) * CH2, CH2), CH2)]

    def step_of(slot):
        n = cfg.step

        def body(i, _):
            r = pl.ds(pl.multiple_of(i * n, n), n)
            g = gbuf[slot, r].astype(F32).reshape(n // 8, 8, 128) * factor[...][None]
            w = wbuf[slot, r].astype(F32).reshape(n // 8, 8, 128)
            m = 0.9 * mbuf[slot, r].reshape(n // 8, 8, 128) + 0.1 * g
            v = 0.95 * vbuf[slot, r].reshape(n // 8, 8, 128) + 0.05 * g * g
            new = w - 0.02 * (m * lax.rsqrt(v + 1e-8) + 0.1 * w)
            nbuf[slot, r] = new.reshape(n, 128).astype(BF16)
            return 0

        lax.fori_loop(0, CH2 // n, body, 0)

    def to_partner(t, dev, sem):
        return remote(at(t, dev), at(t, dev), sem, pr2.at[t // (2 * K2)], partner)

    def own_to_partner(t):
        slot = lax.rem(t, 2)
        return remote(nbuf.at[slot], at(t, me), pown_sem.at[slot], pr2.at[t // (2 * K2)], partner)

    def own_to_wt(t):
        slot = lax.rem(t, 2)
        return pltpu.make_async_copy(nbuf.at[slot], at(t, me), loc_sem.at[slot])

    def end_send(u):
        return remote(at(u - M, me), at(u - M, me), e_sem.at[lax.rem(u, 2)], re.at[u - M], to_c)

    def end_phase(t, _):
        @pl.when(t < M)
        def _():
            slot = lax.rem(t, 2)

            @pl.when(t >= 2)
            def _():
                hand(t - 2).wait_send()

            @pl.when(t >= 1)
            def _():
                hand(t).start()

            @pl.when(t + 1 < M)
            def _():
                loads(t + 1, 1 - slot)
                load_g(t + 1, 1 - slot).start()

            wait_loads(slot)
            load_g(t, slot).wait()

            @pl.when(t >= 2)
            def _():
                own_to_wt(t - 2).wait()
                own_to_partner(t - 2).wait_send()

            step_of(slot)
            own_to_wt(t).start()
            own_to_partner(t).start()

            @pl.when(t == M - 1)
            def _():
                for j in (M - 2, M - 1):
                    own_to_wt(jnp.int32(j)).wait()
                    own_to_partner(jnp.int32(j)).wait_send()

        @pl.when((t >= M) & (t < 2 * M))
        def _():
            @pl.when(t < M + 2)
            def _():
                hand(t - 2).wait_send()

            @pl.when(t >= M + 2)
            def _():
                end_send(t - 2).wait_send()

            end_send(t).start()

        @pl.when((t >= 2 * M) & (t < 2 * M + 2))
        def _():
            end_send(t - 2).wait_send()

        q = t - L

        @pl.when(q >= 0)
        def _():
            c, j = q // M, lax.rem(q, M)
            dev = 2 * jnp.where(c == 0, my_mid, jnp.where(c == 1, far_mid, far_end)) + k
            remote(at(j, dev), at(j, dev), pfc.at[0], rc.at[q], partner).wait_recv()

            @pl.when(q >= 2)
            def _():
                to_partner(j, dev, pfc.at[lax.rem(q, 2)]).wait_send()

            to_partner(j, dev, pfc.at[lax.rem(q, 2)]).start()

        return 0

    def mid_own(t, there):
        slot = lax.rem(t, 2)
        if there == "e":
            return remote(nbuf.at[slot], at(t, me), e_sem.at[slot], rc.at[t], to_e)
        return remote(nbuf.at[slot], at(t, me), c_sem.at[slot], rc.at[t], to_c)

    def mid_to_end(u):
        j = lax.rem(u, M)
        dev = 2 * jnp.where(u < 2 * M, far_mid, far_end) + k
        return remote(at(j, dev), at(j, dev), e_sem.at[lax.rem(u, 2)], rc.at[u], to_e)

    def mid_across(q):
        dev = 2 * my_end + k
        return remote(at(q, dev), at(q, dev), c_sem.at[lax.rem(q, 2)], rc.at[M + q], to_c)

    def mid_phase(t, _):
        @pl.when(t < M)
        def _():
            slot = lax.rem(t, 2)

            @pl.when(t + 1 < M)
            def _():
                loads(t + 1, 1 - slot)

            hand(t).wait_recv()
            load_g(t, slot).start()
            wait_loads(slot)
            load_g(t, slot).wait()

            @pl.when(t >= 2)
            def _():
                own_to_wt(t - 2).wait()
                own_to_partner(t - 2).wait_send()
                mid_own(t - 2, "e").wait_send()
                mid_own(t - 2, "c").wait_send()

            step_of(slot)
            mid_own(t, "e").start()
            mid_own(t, "c").start()
            own_to_partner(t).start()
            own_to_wt(t).start()

        @pl.when((t >= M) & (t < M + 2))
        def _():
            own_to_wt(t - 2).wait()
            own_to_partner(t - 2).wait_send()
            mid_own(t - 2, "e").wait_send()
            mid_own(t - 2, "c").wait_send()

        @pl.when((t >= M) & (t < 3 * M))
        def _():
            @pl.when(t >= M + 2)
            def _():
                mid_to_end(t - 2).wait_send()

            mid_to_end(t).start()

        @pl.when(t >= 3 * M)
        def _():
            @pl.when(t < 3 * M + 2)
            def _():
                mid_to_end(t - 2).wait_send()

        e = t - M - L

        @pl.when((e >= 0) & (e < M))
        def _():
            dev = 2 * my_end + k
            remote(at(e, dev), at(e, dev), pfe.at[0], re.at[e], partner).wait_recv()

            @pl.when(e >= 2)
            def _():
                to_partner(e, dev, pfe.at[lax.rem(e, 2)]).wait_send()
                mid_across(e - 2).wait_send()

            mid_across(e).start()
            to_partner(e, dev, pfe.at[lax.rem(e, 2)]).start()

        @pl.when((e >= M) & (e < M + 2))
        def _():
            to_partner(e - 2, 2 * my_end + k, pfe.at[lax.rem(e, 2)]).wait_send()
            mid_across(e - 2).wait_send()

        q = t - 2 * L

        @pl.when((q >= 0) & (q < 2 * M))
        def _():
            j = lax.rem(q, M)
            dev = 2 * jnp.where(q < M, far_mid, far_end) + k
            remote(at(j, dev), at(j, dev), pfc.at[0], rc.at[q], partner).wait_recv()

            @pl.when(q >= 2)
            def _():
                to_partner(j, dev, pfc.at[lax.rem(q, 2)]).wait_send()

            to_partner(j, dev, pfc.at[lax.rem(q, 2)]).start()

        return 0

    @pl.when(end)
    def _():
        lax.fori_loop(0, 3 * M + L, end_phase, 0)

    @pl.when(mid)
    def _():
        lax.fori_loop(0, 3 * M + 2, mid_phase, 0)

    for j in range(2):
        to_partner(jnp.int32(0), me, pfc.at[j]).wait_send()
    for s in (0, 1):
        for i in range(N - SP, N):
            wait_given(s, jnp.int32(i))

    @pl.when(end)
    def _():
        for i in range(1, 8):
            tell(i).wait_send()

    for w in range(3):
        half_of = wt.at[w, :, pl.ds(0, 4 * R)]
        pltpu.make_async_copy(half_of, half_of, pr2.at[w]).wait()


def sum_step_gather(cfg, terms, weights, m, v):
    R, DMA, REG = cfg.R, pltpu.SemaphoreType.DMA, pltpu.SemaphoreType.REGULAR
    CH, CH2, SL, SP, SR, SO, M = cfg.CH, cfg.CH2, cfg.SL, cfg.SP, cfg.SR, cfg.SO, cfg.M
    anywhere = pl.BlockSpec(memory_space=pl.ANY)
    return pl.pallas_call(
        functools.partial(kernel, cfg),
        name="sum_step_gather",
        out_shape=(
            jax.ShapeDtypeStruct((3, 2, 8 * R, 128), BF16),
            jax.ShapeDtypeStruct((3, 2, R, 128), BF16),
            jax.ShapeDtypeStruct((3, 2, R, 128), BF16),
            jax.ShapeDtypeStruct((8, 128), F32),
        ),
        in_specs=[anywhere] * 12,
        out_specs=(anywhere, anywhere, anywhere, pl.BlockSpec(memory_space=pltpu.VMEM)),
        scratch_shapes=[
            pltpu.VMEM((2, SL, CH, 128), BF16),
            pltpu.VMEM((2, SP, CH, 128), BF16),
            pltpu.VMEM((2, SR, CH, 128), BF16),
            pltpu.VMEM((2, SO, CH, 128), BF16),
            pltpu.VMEM((8, 128), F32),
            pltpu.VMEM((4, 8, 128), F32),
            pltpu.VMEM((2, CH2, 128), BF16),
            pltpu.VMEM((2, CH2, 128), BF16),
            pltpu.VMEM((2, CH2, 128), F32),
            pltpu.VMEM((2, CH2, 128), F32),
            pltpu.VMEM((2, CH2, 128), BF16),
            DMA((2, SL)),
            DMA((2, SP)),
            DMA((2, SP)),
            DMA((2, SO)),
            DMA((2, SR)),
            REG((2,)),
            REG((2,)),
            DMA((8,)),
            DMA((4,)),
            DMA((2,)),
            DMA((2,)),
            DMA((2,)),
            DMA((2,)),
            DMA((2,)),
            DMA((2,)),
            DMA((3,)),
            DMA((M,)),
            DMA((M,)),
            DMA((3 * M,)),
            DMA((3, 2)),
            DMA((2,)),
        ],
        compiler_params=pltpu.CompilerParams(collective_id=0, has_side_effects=True, vmem_limit_bytes=60 * 2**20),
    )(*terms, *weights, *m, *v)


def solution(mesh):
    def step(*arrays):
        terms, weights, m, v = (arrays[i : i + 3] for i in (0, 3, 6, 9))
        rows = m[0].shape[1] * m[0].shape[2] // 128
        cfg = Cfg(rows, ch=rows // 16, skew=3, ch2=rows // 4, lag=4)
        cfg.step = min(cfg.CH, 80)
        wt, g_own, _, factor = sum_step_gather(
            cfg,
            [rows_of(t[0]) for t in terms],
            [rows_of(w) for w in weights],
            [rows_of(x) for x in m],
            [rows_of(x) for x in v],
        )
        whole = [from_rows(wt[j], *w.shape[1:]) for j, w in enumerate(weights)]
        new_m, new_v = [], []
        for j in range(3):
            g = from_rows(g_own[j], *m[j].shape[1:]).astype(F32) * factor[0, 0]
            new_m.append(0.9 * m[j] + 0.1 * g)
            new_v.append(0.95 * v[j] + 0.05 * g * g)
        return (*whole, *new_m, *new_v)

    all_of, cut = P(None, None, None), P(None, "dp", None)
    return jax.shard_map(
        step,
        mesh=mesh,
        in_specs=(P(("rep", "dp"), None, None, None),) * 3 + (all_of,) * 3 + (cut,) * 6,
        out_specs=(P("rep", None, None),) * 3 + (P("rep", "dp", None),) * 6,
        check_vma=False,
    )
```

time: 1570 us -> 1180 us (0.75)
  waiting for transfers between devices: 1430 us -> 0 us
  Pallas kernels: 0 us -> 1090 us
  between operations: 16.8 us -> 0.66 us
    pallas_call x0 -> x1, Pallas kernels: none -> 1090 us  [sum_step_gather(): pl.pallas_call(functools.partial(kernel, cfg), name='sum_step_gather', ou...]
    reduce_scatter x3 -> x0, waiting for transfers between devices: 766 us -> none  [step(): lax.psum_scatter(t[0], 'dp', scatter_dimension=1, tiled=True)]
    all_gather x3 -> x0, waiting for transfers between devices: 662 us -> none  [step(): whole = [lax.all_gather(one[0], 'dp', axis=1, tiled=True) for one in new]]
    slice x0 -> x2, local copies, waits for them, and re-layouts: none -> 52.9 us  [the longest x1 51.7 us: step(): whole = [from_rows(wt[j], *w.shape[1:]) for j, w in enumerate(weights)]]
    unnamed x7 -> x4, local copies, waits for them, and re-layouts: 53.4 us -> 1.51 us
    convert_element_type x3 -> x0, other arithmetic: 38.4 us -> none  [adamw(): return ((w - 0.02 * step).astype(jnp.bfloat16), m, v)]
    add x0 -> x2, other arithmetic: none -> 28.7 us  [step(): new_v.append(0.95 * v[j] + 0.05 * g * g)]
  transfers between devices with their start and end apart: 6 -> 0, of which waited for: 6 -> 0; matrix products, arithmetic and copies ran while one was open for 2% -> 0% of each run, Pallas kernels for 0% -> 0%
where the time goes in v1:
time: 1180 us
  Pallas kernels  1090 us (92%)
  local copies, waits for them, and re-layouts  54.4 us (5%)
  other arithmetic  39.4 us (3%)
    pallas_call x1, Pallas kernels, sum_step_gather(): pl.pallas_call(functools.partial(kernel, cfg), name='sum_step_gather', ou...  1090 us
    slice x1, local copies, waits for them, and re-layouts, step(): whole = [from_rows(wt[j], *w.shape[1:]) for j, w in enumerate(weights)]  51.7 us
    add x2, other arithmetic, step(): new_v.append(0.95 * v[j] + 0.05 * g * g)  28.7 us

profile of v1, /device:TPU:0, one launch (start us, length us, event | category | flops | bytes accessed | tf_op | source)
XLA Modules:
  0.0 1179.9 jit_solution(17987389969809483833)
XLA Ops:
  0.6 1085.5 %sum_step_gather.1 = (bf16[3,2,51200,128]{3,2,1,0:T(8,128)(2,1)}, bf16[3,2,6400,128]{3,2,1,0:T(8,128)(2,1)}, bf16[3,2,6400,128]{3,2,1,0:T(8,128)(2,1)}, f32[8,128]{1,0:T(8,128)}) custom-call(bf16[2,51200,128]{2,1,0:T(8,128)(2,1)} %bitcast.91, bf16[2,51200,128]{2,1,0:T(8,128)(2,1)} %bitcast.92, bf16[2,51200,128]{2,1,0:T(8,128)(2,1)} %bitcast.93, ...), custom_call_target="tpu_custom_call" | custom-call | tf_op jit(solution)/shard_map/sum_step_gather/pallas_call | solution.py:519
  1086.1 1.2 slice.27
  1087.3 51.7 %fusion.3 = (bf16[1,2,51200,128]{3,2,1,0:T(8,128)(2,1)}, bf16[1,2,51200,128]{3,2,1,0:T(8,128)(2,1)}, bf16[1,2,51200,128]{3,2,1,0:T(8,128)(2,1)}) fusion(bf16[3,2,51200,128]{3,2,1,0:T(8,128)(2,1)} %get-tuple-element.12), kind=kLoop, calls=%fused_computation.12 | loop fusion | bytes 157286400 | tf_op jit(solution)/shard_map/slice | solution.py:581
  1139.0 0.0 copy-start
  1139.0 0.0 copy-start.1
  1139.0 10.7 convert_multiply_fusion
  1149.7 0.0 copy-done
  1149.7 1.5 copy-done.1
  1151.2 5.8 fusion.2
  1157.0 22.9 %fusion = (f32[2,160,5120]{2,1,0:T(8,128)}, f32[2,160,5120]{2,1,0:T(8,128)}, f32[2,160,5120]{2,1,0:T(8,128)}, f32[2,160,5120]{2,1,0:T(8,128)}) fusion(f32[2,160,5120]{2,1,0:T(8,128)} %bitcast.104, f32[2,160,5120]{2,1,0:T(8,128)} %param.21, f32[2,160,5120]{2,1,0:T(8,128)} %param.18, f32[2,160,5120]{2,1,0:T(8,128)} %bitcast.103, f32[2,160,5120]{2,1,0:T(8,128)} %param.19, ...), kind=kLoop, calls=%fused_computation.3 | loop fusion | flops 22937600 | bytes 65536000 | tf_op jit(solution)/shard_map/add | solution.py:586
Async XLA Ops:
  1139.0 10.7 copy-start
  1139.0 12.2 %copy-start.1 = (f32[2,640,1280]{2,1,0:T(8,128)S(1)}, f32[2,640,1280]{2,1,0:T(8,128)}, u32[]{:S(2)}) copy-start(f32[2,640,1280]{2,1,0:T(8,128)} %param.23) | copy-start | bytes 19660804

commit v2 on v1

--- a/solution.py
+++ b/solution.py
@@ -54,11 +54,14 @@
     lax.fori_loop(0, n // step, body, 0)
 
 
-def kernel(cfg, g0, g1, g2, w0, w1, w2, m0, m1, m2, v0, v1, v2, wt, g_own, g_fwd, factor, own, par, rin, out, sq, sq_in,
+def kernel(cfg, g0, g1, g2, w0, w1, w2, m0, m1, m2, v0, v1, v2, wt, g_own, g_fwd, factor, late0, late1, plate0, plate1, own, par, rin, out, sq, sq_in,
            gbuf, wbuf, mbuf, vbuf, nbuf, own_sem, ps, pr, rs, rr, par_credit, rin_credit, sqs, sqr,
-           e_sem, c_sem, loc_sem, pown_sem, pfc, pfe, pr2, g1r, re, rc, ld_sem, gl_sem):
+           e_sem, c_sem, loc_sem, pown_sem, pfc, pfe, pr2, plr, g1r, re, rc, ld_sem, gl_sem):
     R, CH, D, SUB, N = cfg.R, cfg.CH, cfg.D, cfg.SUB, cfg.N
     SL, SP, SR, SO, CH2, K2, M, L = cfg.SL, cfg.SP, cfg.SR, cfg.SO, cfg.CH2, cfg.K2, cfg.M, cfg.L
+    late, plate = (late0, late1), (plate0, plate1)
+    T = 2 * K2
+    first_late = M - T
     g_in, w_in, m_in, v_in = (g0, g1, g2), (w0, w1, w2), (m0, m1, m2), (v0, v1, v2)
     me = lax.axis_index("dp")
     chip, k = me // 2, lax.rem(me, 2)
@@ -310,6 +313,13 @@
     def to_partner(t, dev, sem):
         return remote(at(t, dev), at(t, dev), sem, pr2.at[t // (2 * K2)], partner)
 
+    def late_at(refs, j, do):
+        off = pl.multiple_of(lax.rem(j, K2) * CH2, CH2)
+        for l in range(2):
+            @pl.when((j - first_late) // K2 == l)
+            def _():
+                do([r[l].at[pl.ds(off, CH2)] for r in refs])
+
     def own_to_partner(t):
         slot = lax.rem(t, 2)
         return remote(nbuf.at[slot], at(t, me), pown_sem.at[slot], pr2.at[t // (2 * K2)], partner)
@@ -400,9 +410,9 @@
         dev = 2 * jnp.where(u < 2 * M, far_mid, far_end) + k
         return remote(at(j, dev), at(j, dev), e_sem.at[lax.rem(u, 2)], rc.at[u], to_e)
 
-    def mid_across(q):
+    def mid_across(q, place=None):
         dev = 2 * my_end + k
-        return remote(at(q, dev), at(q, dev), c_sem.at[lax.rem(q, 2)], rc.at[M + q], to_c)
+        return remote(at(q, dev), at(q, dev) if place is None else place, c_sem.at[lax.rem(q, 2)], rc.at[M + q], to_c)
 
     def mid_phase(t, _):
         @pl.when(t < M)
@@ -438,7 +448,7 @@
             mid_own(t - 2, "e").wait_send()
             mid_own(t - 2, "c").wait_send()
 
-        @pl.when((t >= M) & (t < 3 * M))
+        @pl.when((t >= M) & (t < 3 * M - T))
         def _():
             @pl.when(t >= M + 2)
             def _():
@@ -446,11 +456,9 @@
 
             mid_to_end(t).start()
 
-        @pl.when(t >= 3 * M)
-        def _():
-            @pl.when(t < 3 * M + 2)
-            def _():
-                mid_to_end(t - 2).wait_send()
+        @pl.when((t >= 3 * M - T) & (t < 3 * M - T + 2))
+        def _():
+            mid_to_end(t - 2).wait_send()
 
         e = t - M - L
 
@@ -464,7 +472,14 @@
                 to_partner(e, dev, pfe.at[lax.rem(e, 2)]).wait_send()
                 mid_across(e - 2).wait_send()
 
-            mid_across(e).start()
+            @pl.when(e < first_late)
+            def _():
+                mid_across(e).start()
+
+            @pl.when(e >= first_late)
+            def _():
+                late_at([late], e, lambda p: mid_across(e, p[0]).start())
+
             to_partner(e, dev, pfe.at[lax.rem(e, 2)]).start()
 
         @pl.when((e >= M) & (e < M + 2))
@@ -478,23 +493,30 @@
         def _():
             j = lax.rem(q, M)
             dev = 2 * jnp.where(q < M, far_mid, far_end) + k
+            sem = pfc.at[lax.rem(q, 2)]
             remote(at(j, dev), at(j, dev), pfc.at[0], rc.at[q], partner).wait_recv()
 
             @pl.when(q >= 2)
             def _():
-                to_partner(j, dev, pfc.at[lax.rem(q, 2)]).wait_send()
-
-            to_partner(j, dev, pfc.at[lax.rem(q, 2)]).start()
+                to_partner(j, dev, sem).wait_send()
+
+            @pl.when(q < 2 * M - T)
+            def _():
+                to_partner(j, dev, sem).start()
+
+            @pl.when(q >= 2 * M - T)
+            def _():
+                late_at([late, plate], j, lambda p: remote(p[0], p[1], sem, plr.at[0], partner).start())
 
         return 0
 
     @pl.when(end)
     def _():
-        lax.fori_loop(0, 3 * M + L, end_phase, 0)
+        lax.fori_loop(0, 3 * M - T + L, end_phase, 0)
 
     @pl.when(mid)
     def _():
-        lax.fori_loop(0, 3 * M + 2, mid_phase, 0)
+        lax.fori_loop(0, max(3 * M - T + 2, 2 * M + 2 * L), mid_phase, 0)
 
     for j in range(2):
         to_partner(jnp.int32(0), me, pfc.at[j]).wait_send()
@@ -508,8 +530,95 @@
             tell(i).wait_send()
 
     for w in range(3):
-        half_of = wt.at[w, :, pl.ds(0, 4 * R)]
-        pltpu.make_async_copy(half_of, half_of, pr2.at[w]).wait()
+        all_given = wt.at[w, :, pl.ds(0, (4 if w < 2 else 3) * R)]
+        pltpu.make_async_copy(all_given, all_given, pr2.at[w]).wait()
+
+    @pl.when(mid)
+    def _():
+        given = wt.at[0, :, pl.ds(0, R)]
+        pltpu.make_async_copy(given, given, plr.at[0]).wait()
+
+
+def outputs(rows, factor, wt, g, m, v, w_out, m_out, v_out):
+    w_out[...] = wt[...]
+
+    def body(i, _):
+        r = pl.ds(pl.multiple_of(i * rows, rows), rows)
+        grad = g[r].astype(F32).reshape(rows // 8, 8, 128) * factor[...][None]
+        new_m = 0.9 * m[r].reshape(rows // 8, 8, 128) + 0.1 * grad
+        new_v = 0.95 * v[r].reshape(rows // 8, 8, 128) + 0.05 * grad * grad
+        m_out[r] = new_m.reshape(rows, 128)
+        v_out[r] = new_v.reshape(rows, 128)
+        return 0
+
+    lax.fori_loop(0, g.shape[0] // rows, body, 0)
+
+
+def write_outputs(cfg, j, factor, wt, g_own, m, v):
+    R = cfg.R
+    parts = 8
+
+    def share(n, *lead):
+        return pl.BlockSpec((*(None,) * (len(lead) + 1), n, 128), lambda l, i: (*lead, l, i, 0))
+
+    big, small = R, R // parts
+    moment = jax.ShapeDtypeStruct((2, R, 128), F32)
+    return pl.pallas_call(
+        functools.partial(outputs, cfg.step),
+        name="write_outputs",
+        grid=(2, parts),
+        in_specs=[pl.BlockSpec((8, 128), lambda l, i: (0, 0)), share(big, j), share(small, j), share(small), share(small)],
+        out_specs=(share(big), share(small), share(small)),
+        out_shape=(jax.ShapeDtypeStruct((2, 8 * R, 128), BF16), moment, moment),
+        cost_estimate=pl.CostEstimate(flops=2 * 10**10, bytes_accessed=(64 + 2 * 18) * R * 128, transcendentals=0),
+    )(factor, wt, g_own, m, v)
+
+
+def insert(layer, R, here, given, mine, yours, _, w_out, buf, ld, st):
+    me = lax.axis_index("dp")
+    chip, k = me // 2, lax.rem(me, 2)
+    end = (chip == 0) | (chip == 3)
+    far_end = 3 - 3 * (chip // 2)
+    n, c = 4, R // 4
+    steps = [(s, i) for i in range(n) for s in range(2)]
+
+    def load(ref, s, i):
+        return pltpu.make_async_copy(ref.at[pl.ds(i * c, c)], buf.at[s, pl.ds(i * c, c)], ld.at[s, i])
+
+    def store(s, i):
+        dev = 2 * far_end + (k if s == 0 else 1 - k)
+        return pltpu.make_async_copy(buf.at[s, pl.ds(i * c, c)], w_out.at[layer, pl.ds(pl.multiple_of(dev * R + i * c, c), c)], st.at[s, i])
+
+    @pl.when(end)
+    def _():
+        for s, i in steps:
+            load((here, given)[s], s, i).start()
+
+    @pl.when(jnp.logical_not(end))
+    def _():
+        for s, i in steps:
+            load((mine, yours)[s], s, i).start()
+
+    for s, i in steps:
+        load(here, s, i).wait()
+        store(s, i).start()
+    for s, i in steps:
+        store(s, i).wait()
+
+
+def insert_late(cfg, layer, here, given, mine, yours, whole):
+    R = cfg.R
+    anywhere = pl.BlockSpec(memory_space=pl.ANY)
+    return pl.pallas_call(
+        functools.partial(insert, layer, R),
+        name="insert_late",
+        in_specs=[anywhere] * 5,
+        out_specs=anywhere,
+        out_shape=jax.ShapeDtypeStruct(whole.shape, whole.dtype),
+        scratch_shapes=[pltpu.VMEM((2, R, 128), BF16), pltpu.SemaphoreType.DMA((2, 4)), pltpu.SemaphoreType.DMA((2, 4))],
+        input_output_aliases={4: 0},
+        cost_estimate=pl.CostEstimate(flops=10**9, bytes_accessed=8 * R * 128, transcendentals=0),
+    )(here, given, mine, yours, whole)
 
 
 def sum_step_gather(cfg, terms, weights, m, v):
@@ -524,9 +633,10 @@
             jax.ShapeDtypeStruct((3, 2, R, 128), BF16),
             jax.ShapeDtypeStruct((3, 2, R, 128), BF16),
             jax.ShapeDtypeStruct((8, 128), F32),
+            *[jax.ShapeDtypeStruct((R, 128), BF16)] * 4,
         ),
         in_specs=[anywhere] * 12,
-        out_specs=(anywhere, anywhere, anywhere, pl.BlockSpec(memory_space=pltpu.VMEM)),
+        out_specs=(anywhere, anywhere, anywhere, pl.BlockSpec(memory_space=pltpu.VMEM), *[anywhere] * 4),
         scratch_shapes=[
             pltpu.VMEM((2, SL, CH, 128), BF16),
             pltpu.VMEM((2, SP, CH, 128), BF16),
@@ -555,6 +665,7 @@
             DMA((2,)),
             DMA((2,)),
             DMA((3,)),
+            DMA((1,)),
             DMA((M,)),
             DMA((M,)),
             DMA((3 * M,)),
@@ -571,19 +682,20 @@
         rows = m[0].shape[1] * m[0].shape[2] // 128
         cfg = Cfg(rows, ch=rows // 16, skew=3, ch2=rows // 4, lag=4)
         cfg.step = min(cfg.CH, 80)
-        wt, g_own, _, factor = sum_step_gather(
-            cfg,
-            [rows_of(t[0]) for t in terms],
-            [rows_of(w) for w in weights],
-            [rows_of(x) for x in m],
-            [rows_of(x) for x in v],
+        rm, rv = [rows_of(x) for x in m], [rows_of(x) for x in v]
+        wt, g_own, _, factor, late0, late1, plate0, plate1 = sum_step_gather(
+            cfg, [rows_of(t[0]) for t in terms], [rows_of(w) for w in weights], rm, rv
         )
-        whole = [from_rows(wt[j], *w.shape[1:]) for j, w in enumerate(weights)]
-        new_m, new_v = [], []
-        for j in range(3):
-            g = from_rows(g_own[j], *m[j].shape[1:]).astype(F32) * factor[0, 0]
-            new_m.append(0.9 * m[j] + 0.1 * g)
-            new_v.append(0.95 * v[j] + 0.05 * g * g)
+        to_end, swap = [(2, 0), (3, 1), (4, 6), (5, 7)], [(0, 1), (1, 0), (6, 7), (7, 6)]
+        here = [lax.ppermute(x, "dp", to_end) for x in (late0, late1)]
+        new = [write_outputs(cfg, j, factor, wt, g_own, rm[j], rv[j]) for j in range(3)]
+        given = [lax.ppermute(x, "dp", swap) for x in here]
+        down = new[2][0]
+        for l, (mine, yours) in enumerate(((late0, plate0), (late1, plate1))):
+            down = insert_late(cfg, l, here[l], given[l], mine, yours, down)
+        whole = [from_rows(x, *w.shape[1:]) for x, w in zip((new[0][0], new[1][0], down), weights, strict=True)]
+        new_m = [from_rows(one[1], *x.shape[1:]) for one, x in zip(new, m, strict=True)]
+        new_v = [from_rows(one[2], *x.shape[1:]) for one, x in zip(new, v, strict=True)]
         return (*whole, *new_m, *new_v)
 
     all_of, cut = P(None, None, None), P(None, "dp", None)

time: 1180 us -> 1130 us (0.958)
  local copies, waits for them, and re-layouts: 54.4 us -> 0.01 us
  other arithmetic: 39.4 us -> 0 us
  Pallas kernels: 1090 us -> 1110 us
    pallas_call x0 -> x5, Pallas kernels: none -> 99.4 us  [the longest x3 93.7 us: write_outputs(): pl.pallas_call(functools.partial(outputs, cfg.step), name='write_outputs'...]
    pallas_call x1, Pallas kernels: 1090 us -> 1020 us  [sum_step_gather(): pl.pallas_call(functools.partial(kernel, cfg), name='sum_step_gather', ou...]
    slice x2 -> x0, local copies, waits for them, and re-layouts: 52.9 us -> none  [the longest x1 51.7 us: step(): whole = [from_rows(wt[j], *w.shape[1:]) for j, w in enumerate(weights)]]
    add x2 -> x0, other arithmetic: 28.7 us -> none  [step(): new_v.append(0.95 * v[j] + 0.05 * g * g)]
  transfers between devices with their start and end apart: 0 -> 4, of which waited for: 0 -> 1; matrix products, arithmetic and copies ran while one was open for 0% -> 0% of each run, Pallas kernels for 0% -> 9%
where the time goes in v2:
time: 1130 us
  Pallas kernels  1110 us (98%)
    pallas_call x1, Pallas kernels, sum_step_gather(): pl.pallas_call(functools.partial(kernel, cfg), name='sum_step_gather', ou...  1020 us
    pallas_call x3, Pallas kernels, write_outputs(): pl.pallas_call(functools.partial(outputs, cfg.step), name='write_outputs'...  93.7 us
  transfers between devices with their start and end apart: 4, of which 1 were waited for; matrix products, arithmetic and copies ran while one was open for 0% of the time, Pallas kernels for 9%

profile of v2, /device:TPU:0, one launch (start us, length us, event | category | flops | bytes accessed | tf_op | source)
XLA Modules:
  0.0 1129.8 jit_solution(7361362923645946166)
XLA Ops:
  0.6 1015.3 %sum_step_gather.1 = (bf16[3,2,51200,128]{3,2,1,0:T(8,128)(2,1)}, bf16[3,2,6400,128]{3,2,1,0:T(8,128)(2,1)}, bf16[3,2,6400,128]{3,2,1,0:T(8,128)(2,1)}, f32[8,12...) custom-call(bf16[2,51200,128]{2,1,0:T(8,128)(2,1)} %bitcast.106, ...), custom_call_target="tpu_custom_call" | custom-call | tf_op jit(solution)/shard_map/sum_step_gather/pallas_call | solution.py:628
  1015.9 1.3 collective-permute-start.2
  1017.2 1.3 collective-permute-start
  1018.5 31.2 %write_outputs.5 = (bf16[2,51200,128]{2,1,0:T(8,128)(2,1)}, f32[2,6400,128]{2,1,0:T(8,128)}, f32[2,6400,128]{2,1,0:T(8,128)}) custom-call(f32[8,128]{1,0:T(8,128)} %get-tuple-element.25.factor, bf16[3,2,51200,128]{3,2,1,0:T(8,128)(2,1)} %get-tuple-element.26.wt, bf16[3,2,6400,128]{3,2,1,0:T(8,128)(2,1)} %get-tuple-element.27.g, f32[2,6400,128]{2,1,0:T(8,128)} %bitcast.113, ...), custom_call_target="tpu_custom_call" | custom-call | flops 20000000000 | bytes 81920000 | tf_op jit(solution)/shard_map/write_outputs/pallas_call | solution.py:566
  1049.7 31.2 %write_outputs.4 = (bf16[2,51200,128]{2,1,0:T(8,128)(2,1)}, f32[2,6400,128]{2,1,0:T(8,128)}, f32[2,6400,128]{2,1,0:T(8,128)}) custom-call(f32[8,128]{1,0:T(8,128)} %get-tuple-element.25.factor, bf16[3,2,51200,128]{3,2,1,0:T(8,128)(2,1)} %get-tuple-element.26.wt, bf16[3,2,6400,128]{3,2,1,0:T(8,128)(2,1)} %get-tuple-element.27.g, f32[2,6400,128]{2,1,0:T(8,128)} %bitcast.117, ...), custom_call_target="tpu_custom_call" | custom-call | flops 20000000000 | bytes 81920000 | tf_op jit(solution)/shard_map/write_outputs/pallas_call | solution.py:566
  1080.9 0.0 collective-permute-done.2.here
  1081.0 0.0 copy-start.1
  1081.0 2.2 collective-permute-start.3
  1083.2 7.7 collective-permute-done.here
  1090.9 0.0 copy-start
  1090.9 1.9 collective-permute-start.1
  1092.8 31.2 %write_outputs.3 = (bf16[2,51200,128]{2,1,0:T(8,128)(2,1)}, f32[2,6400,128]{2,1,0:T(8,128)}, f32[2,6400,128]{2,1,0:T(8,128)}) custom-call(f32[8,128]{1,0:T(8,128)} %get-tuple-element.25.factor, bf16[3,2,51200,128]{3,2,1,0:T(8,128)(2,1)} %get-tuple-element.26.wt, bf16[3,2,6400,128]{3,2,1,0:T(8,128)(2,1)} %get-tuple-element.27.g, f32[2,6400,128]{2,1,0:T(8,128)} %bitcast.121, ...), custom_call_target="tpu_custom_call" | custom-call | flops 20000000000 | bytes 81920000 | tf_op jit(solution)/shard_map/write_outputs/pallas_call | solution.py:566
  1124.0 0.0 copy-done.1
  1124.1 0.0 copy-done
  1124.1 0.0 collective-permute-done.3.given
  1124.1 2.9 insert_late.2._
  1126.9 0.0 collective-permute-done.1.given
  1126.9 2.9 insert_late.3
Async XLA Ops:
  1015.9 65.0 %collective-permute-start.2 = (bf16[6400,128]{1,0:T(8,128)(2,1)}, bf16[6400,128]{1,0:T(8,128)(2,1)S(1)}, u32[]{:S(2)}, u32[]{:S(2)}) collective-permute-start(bf16[6400,128]{1,0:T(8,128)(2,1)} %get-tuple-element.32.mine), channel_id=1, source_target_pairs={{2,0},{3,1},{4,6},{5,7},{10,8},{11,9},{12,14},{13,15},{18,16},{19,... | collective-permute-start | bytes 4915208 | tf_op jit(solution)/shard_map/ppermute | solution.py:690
  1017.2 73.7 %collective-permute-start = (bf16[6400,128]{1,0:T(8,128)(2,1)}, bf16[6400,128]{1,0:T(8,128)(2,1)S(1)}, u32[]{:S(2)}, u32[]{:S(2)}) collective-permute-start(bf16[6400,128]{1,0:T(8,128)(2,1)} %get-tuple-element.30.mine), channel_id=1, source_target_pairs={{2,0},{3,1},{4,6},{5,7},{10,8},{11,9},{12,14},{13,15},{18,16},{19,... | collective-permute-start | bytes 4915208 | tf_op jit(solution)/shard_map/ppermute | solution.py:690
  1081.0 43.1 %copy-start.1 = (bf16[6400,128]{1,0:T(8,128)(2,1)}, bf16[6400,128]{1,0:T(8,128)(2,1)S(1)}, u32[]{:S(2)}) copy-start(bf16[6400,128]{1,0:T(8,128)(2,1)S(1)} %collective-permute-done.2.here) | copy-start | bytes 4915204
  1081.0 43.1 %collective-permute-start.3 = (bf16[6400,128]{1,0:T(8,128)(2,1)S(1)}, bf16[6400,128]{1,0:T(8,128)(2,1)}, u32[]{:S(2)}, u32[]{:S(2)}) collective-permute-start(bf16[6400,128]{1,0:T(8,128)(2,1)S(1)} %collective-permute-done.2.here), channel_id=1, source_target_pairs={{0,1},{1,0},{6,7},{7,6},{8,9},{9,8},{14,15},{15,14},{16,17},{17,16... | collective-permute-start | bytes 4915208 | tf_op jit(solution)/shard_map/ppermute | solution.py:692
  1090.9 33.1 %copy-start = (bf16[6400,128]{1,0:T(8,128)(2,1)}, bf16[6400,128]{1,0:T(8,128)(2,1)S(1)}, u32[]{:S(2)}) copy-start(bf16[6400,128]{1,0:T(8,128)(2,1)S(1)} %collective-permute-done.here) | copy-start | bytes 4915204
  1090.9 36.0 %collective-permute-start.1 = (bf16[6400,128]{1,0:T(8,128)(2,1)S(1)}, bf16[6400,128]{1,0:T(8,128)(2,1)}, u32[]{:S(2)}, u32[]{:S(2)}) collective-permute-start(bf16[6400,128]{1,0:T(8,128)(2,1)S(1)} %collective-permute-done.here), channel_id=1, source_target_pairs={{0,1},{1,0},{6,7},{7,6},{8,9},{9,8},{14,15},{15,14},{16,17},{17,16... | collective-permute-start | bytes 4915208 | tf_op jit(solution)/shard_map/ppermute | solution.py:692
